TPU v7x, 32 devices: a whole 2x2x4 slice. The times are simulated.
32 devices in a mesh: seq: 16 (over z, y, core), batch: 2 (over x).
Axes of the slice: x: 2, y: 2, z: 4, core: 2. Of those that a mesh axis runs over, the one named last changes fastest.
Arguments:
- hidden_in: bfloat16 [2, 4096, 2304], P('batch', 'seq'), may hold values from -6 to 6
- segment_ids: int32 [2, 4096], P('batch', 'seq'), may hold values from 0 to 15, never falling along the last dimension, each value on 1 to 512 neighbouring positions
- pre_gain: float32 [2304], replicated, may hold values from 0.25 to 1.75
- w_qkv: bfloat16 [2304, 2048], P('seq'), may hold values from -0.27083333 to 0.27083333
- w_out: bfloat16 [1024, 2304], P('seq'), may hold values from -0.1875 to 0.1875
- post_gain: float32 [2304], replicated, may hold values from 0.25 to 1.75
Outputs:
- layer_out: bfloat16 [2, 4096, 2304], P('batch', 'seq')
Inputs may be any that keep to these rules, and one draw needn't show every extreme that they name: `segment_ids`: along each sequence the numbers never fall; a document is 1 to 512 positions long, and each sequence has one of exactly 512.
All inputs are finite; a program needn't handle non-finite values.
Results may differ from a plain program's by a relative error of at most 0.012.
The roundings to bfloat16 on the way count: a program that leaves them out, or rounds other values in their place, can miss the bound.
Values may be sent and summed in bfloat16 or wider, within the bound.
A program may use at most 128 MiB of HBM per device.

v0:
```python
import math
import jax
import jax.numpy as jnp
from jax import lax
from jax.sharding import PartitionSpec as P

Q_HEADS = 4
KV_HEADS = 2
HEAD = 256
WINDOW = 4096
DOCS = 16
EPS = 1e-06
CAP = 50.0


def from_behind(block, axis, distance):
    devices = range(lax.axis_size(axis))
    route = [(i - distance, i) for i in devices if i - distance in devices]
    return lax.ppermute(block, axis, route)


def rms_scale(values, gain):
    return values * lax.rsqrt(jnp.mean(values * values, axis=-1, keepdims=True) + EPS) * gain


def rotary(values, positions, leading):
    head_size = values.shape[-1]
    half_dim = head_size // 2
    inverse = 1.0 / 10000.0 ** (jnp.arange(half_dim, dtype=jnp.float32) * 2.0 / head_size)
    angles = positions.astype(jnp.float32)[:, None] * inverse[None, :]
    shape = (
        (1,) * leading + (positions.shape[0],) + (1,) * (values.ndim - 2 - leading) + (half_dim,)
    )
    cosine = jnp.cos(angles).reshape(shape)
    sine = jnp.sin(angles).reshape(shape)
    first_half = values[..., :half_dim]
    second_half = values[..., half_dim:]
    return jnp.concatenate(
        [first_half * cosine - second_half * sine, second_half * cosine + first_half * sine],
        axis=-1,
    )


def per_device(hidden_in, segment_ids, pre_gain, w_qkv, w_out, post_gain):
    tok_rows = hidden_in.shape[1]
    seq_count = lax.axis_size("seq")
    seq_index = lax.axis_index("seq")
    groups = Q_HEADS // KV_HEADS
    doc_most = min(WINDOW, seq_count * tok_rows // 8)
    hops = min(-(-(doc_most - 1) // tok_rows), seq_count - 1)
    positions = seq_index * tok_rows + jnp.arange(tok_rows, dtype=jnp.int32)
    own_ids = segment_ids[0]
    id_blocks = [from_behind(own_ids, "seq", d) for d in range(hops, 0, -1)] + [own_ids]
    widened = hidden_in[0].astype(jnp.float32)
    normed = rms_scale(widened, pre_gain).astype(jnp.bfloat16)
    projected = jnp.dot(
        normed, lax.all_gather(w_qkv, "seq", axis=0, tiled=True), preferred_element_type=jnp.float32
    )
    queries = rotary(
        projected[:, : Q_HEADS * HEAD].reshape(tok_rows, KV_HEADS, groups, HEAD), positions, 0
    ).astype(jnp.bfloat16)
    key_rows = rotary(
        projected[:, Q_HEADS * HEAD : (Q_HEADS + KV_HEADS) * HEAD].reshape(
            tok_rows, KV_HEADS, HEAD
        ),
        positions,
        0,
    ).astype(jnp.bfloat16)
    value_rows = projected[:, (Q_HEADS + KV_HEADS) * HEAD :].astype(jnp.bfloat16)
    both = jnp.concatenate([key_rows.reshape(tok_rows, KV_HEADS * HEAD), value_rows], axis=1)
    blocks = [from_behind(both, "seq", d) for d in range(hops, 0, -1)] + [both]
    kv = jnp.concatenate(blocks, axis=0).reshape(-1, 2, KV_HEADS, HEAD)
    ids = jnp.concatenate(id_blocks, axis=0)
    key_pos = (seq_index - hops) * tok_rows + jnp.arange((hops + 1) * tok_rows, dtype=jnp.int32)
    allowed = (
        (key_pos[None, :] >= 0)
        & (key_pos[None, :] <= positions[:, None])
        & (positions[:, None] - key_pos[None, :] < WINDOW)
        & (ids[None, :] == own_ids[:, None])
    )
    scores = jnp.einsum("qhgd,khd->hgqk", queries, kv[:, 0], preferred_element_type=jnp.float32) * (
        1.0 / math.sqrt(HEAD)
    )
    capped = CAP * jnp.tanh(scores / CAP)
    weights = jnp.where(allowed[None, None], jnp.exp(capped), 0.0)
    totals = jnp.sum(weights, axis=-1)
    mixed = jnp.einsum(
        "hgqk,khd->hgqd", weights.astype(jnp.bfloat16), kv[:, 1], preferred_element_type=jnp.float32
    )
    attended = (mixed / totals[..., None]).astype(jnp.bfloat16)
    attended = attended.transpose(2, 0, 1, 3).reshape(tok_rows, Q_HEADS * HEAD)
    branch = jnp.dot(
        attended,
        lax.all_gather(w_out, "seq", axis=0, tiled=True),
        preferred_element_type=jnp.float32,
    )
    return (widened + rms_scale(branch, post_gain)).astype(jnp.bfloat16)[None]


def solution(mesh):
    placed = (P("batch", "seq", None), P("batch", "seq"), P(), P("seq", None), P("seq", None), P())
    return jax.shard_map(
        per_device, mesh=mesh, in_specs=placed, out_specs=P("batch", "seq", None), check_vma=False
    )
```

profile of v0, /device:TPU:17, one launch (start us, length us, event | category | flops | bytes accessed | tf_op | source)
XLA Modules:
  0.0 167.0 jit_solution(11932889768963249122)
XLA Ops:
  6.5 0.7 all-gather.3.cloned.1.call-update
  8.0 3.7 %collective-permute-start.1 = (s32[256]{0:T(256)}, s32[256]{0:T(256)S(1)}, u32[]{:S(2)}, u32[]{:S(2)}) collective-permute-start(s32[256]{0:T(256)} %bitcast.51), channel_id=1, source_target_pairs={{0,2},{2,4},{4,6},{6,8},{8,10},{10,12},{12,14},{14,16},{16,18},{18... | collective-permute-start | bytes 3080 | tf_op jit(solution)/shard_map/ppermute | solution.py:19
  11.7 3.1 %collective-permute-start = (s32[256]{0:T(256)}, s32[256]{0:T(256)S(1)}, u32[]{:S(2)}, u32[]{:S(2)}) collective-permute-start(s32[256]{0:T(256)} %bitcast.52), channel_id=1, source_target_pairs={{0,4},{2,6},{4,8},{6,10},{8,12},{10,14},{12,16},{14,18},{16,20},{1... | collective-permute-start | bytes 3080 | tf_op jit(solution)/shard_map/ppermute | solution.py:19
  14.9 1.6 fusion
  16.5 1.3 multiply_cosine_fusion
  17.8 1.4 fusion.26
  19.2 72.1 %all-gather.3.cloned.1.call-done = bf16[2304,2048]{1,0:T(8,128)(2,1)} async-done(((bf16[144,2048]{1,0:T(8,128)(2,1)}), bf16[2304,2048]{1,0:T(8,128)(2,1)}) %all-gather.3.cloned.1.call-update) | async-done | bytes 9437200 | tf_op jit(solution)/shard_map/all_gather | solution.py:57
  91.3 5.2 %fusion.16 = f32[256,2048]{1,0:T(8,128)S(1)} fusion(bf16[2304,2048]{1,0:T(8,128)(2,1)} %all-gather.3.cloned.1.call-done, bf16[1,256,2304]{2,1,0:T(8,128)(2,1)S(1)} %copy-done, f32[2304]{0:T(1024)S(1)} %copy-done.10, f32[256]{0:T(256)S(1)} %add_rsqrt_fusion.1), kind=kOutput, calls=%fused_computation.19 | convolution fusion | flops 2418278400 | bytes 12724224 | tf_op jit(solution)/shard_map/dot_general | solution.py:56
  96.7 1.4 reshape.256
  98.0 1.4 subtract_convert_fusion.1
  99.8 0.9 pad_maximum_fusion
  100.7 2.4 %collective-permute-start.3 = (bf16[256,1024]{1,0:T(8,128)(2,1)}, bf16[256,1024]{1,0:T(8,128)(2,1)}, u32[]{:S(2)}, u32[]{:S(2)}) collective-permute-start(bf16[256,1024]{1,0:T(8,128)(2,1)} %pad_maximum_fusion), channel_id=1, source_target_pairs={{0,2},{2,4},{4,6},{6,8},{8,10},{10,12},{12,14},{14,16},{16,18},{18... | collective-permute-start | bytes 1572872 | tf_op jit(solution)/shard_map/ppermute | solution.py:19
  103.1 3.2 %collective-permute-start.2 = (bf16[256,1024]{1,0:T(8,128)(2,1)}, bf16[256,1024]{1,0:T(8,128)(2,1)}, u32[]{:S(2)}, u32[]{:S(2)}) collective-permute-start(bf16[256,1024]{1,0:T(8,128)(2,1)} %pad_maximum_fusion), channel_id=1, source_target_pairs={{0,4},{2,6},{4,8},{6,10},{8,12},{10,14},{12,16},{14,18},{16,20},{1... | collective-permute-start | bytes 1572872 | tf_op jit(solution)/shard_map/ppermute | solution.py:19
  106.3 0.9 reshape.258
  107.6 0.9 subtract_convert_fusion
  108.6 5.3 %collective-permute-done.3 = bf16[256,1024]{1,0:T(8,128)(2,1)} collective-permute-done((bf16[256,1024]{1,0:T(8,128)(2,1)}, bf16[256,1024]{1,0:T(8,128)(2,1)}, u32[]{:S(2)}, u32[]{:S(2)}) %collective-permute-start.3) | collective-permute-done | bytes 524320 | tf_op jit(solution)/shard_map/ppermute | solution.py:19
  113.8 32.1 %collective-permute-done.2 = bf16[256,1024]{1,0:T(8,128)(2,1)} collective-permute-done((bf16[256,1024]{1,0:T(8,128)(2,1)}, bf16[256,1024]{1,0:T(8,128)(2,1)}, u32[]{:S(2)}, u32[]{:S(2)}) %collective-permute-start.2) | collective-permute-done | bytes 524320 | tf_op jit(solution)/shard_map/ppermute | solution.py:19
  146.0 1.4 maximum_maximum_fusion
  147.3 1.2 reshape.257
  148.5 2.0 %fusion.35 = (bf16[768,1,2,256]{3,2,1,0:T(2,128)(2,1)S(1)}, bf16[768,1,2,256]{3,2,1,0:T(2,128)(2,1)}) fusion(bf16[768,2,2,256]{3,2,1,0:T(2,128)(2,1)S(1)} %reshape.257), kind=kLoop, calls=%fused_computation.54 | loop fusion | bytes 3145728 | tf_op jit(solution)/shard_map/slice | solution.py:88
  151.1 2.4 %fusion.4 = (f32[2,2,256]{2,1,0:T(2,128)S(1)}, f32[2,768,256,2]{2,1,3,0:T(8,128)S(1)}) fusion(pred[256,768]{0,1:T(8,128)(4,1)} %fusion.26, bf16[256,2,2,128]{3,0,2,1:T(8,128)(2,1)} %get-tuple-element.8, bf16[256,2,2,128]{3,0,2,1:T(8,128)(2,1)S(1)} %copy-done.6, bf16[768,1,2,256]{3,2,1,0:T(2,128)(2,1)} %get-tuple-element.6), kind=kOutput, calls=%fused_computation.9 | convolution fusion | flops 406846464 | bytes 4657152 | tf_op jit(solution)/shard_map/qhgd,khd->hgqk/dot_general | solution.py:81
  153.5 1.2 divide_convert_fusion
  154.7 4.0 %multiply_reduce_fusion = (f32[256]{0:T(256)S(1)}, f32[256,2304]{1,0:T(8,128)S(1)}) fusion(bf16[256,1024]{0,1:T(8,128)(2,1)S(1)} %bitcast.49, bf16[1024,2304]{1,0:T(8,128)(2,1)} %all-gather.5.cloned.1.call-done), kind=kOutput, calls=%fused_computation.8 | convolution fusion | flops 1209138944 | bytes 7603200 | tf_op jit(solution)/shard_map/dot_general | solution.py:92
  158.7 1.4 fusion.15
  (44 shorter events, 2.2 us)
Async XLA Ops:
  6.5 11.3 %copy-start.9 = (s32[1,256]{1,0:T(1,128)S(1)}, s32[1,256]{1,0:T(1,128)}, u32[]{:S(2)}) copy-start(s32[1,256]{1,0:T(1,128)} %param.7) | copy-start | bytes 3076
  6.5 84.8 %copy-start = (bf16[1,256,2304]{2,1,0:T(8,128)(2,1)S(1)}, bf16[1,256,2304]{2,1,0:T(8,128)(2,1)}, u32[]{:S(2)}) copy-start(bf16[1,256,2304]{2,1,0:T(8,128)(2,1)} %param.6) | copy-start | bytes 3538948
  6.5 84.8 %copy-start.10 = (f32[2304]{0:T(1024)S(1)}, f32[2304]{0:T(1024)}, u32[]{:S(2)}) copy-start(f32[2304]{0:T(1024)} %param.8) | copy-start | bytes 27652
  6.5 84.8 %all-gather.3.cloned.1.call-start = ((), (), s32[]{:S(2)}) async-start(), calls=%async_computation | async-start | bytes 10027008 | tf_op jit(solution)/shard_map/all_gather | solution.py:57
  7.3 147.4 %all-gather.5.cloned.1.call-start = ((), (), s32[]{:S(2)}) async-start(), calls=%async_computation.1 | async-start | bytes 5013504 | tf_op jit(solution)/shard_map/all_gather | solution.py:94
  8.0 9.8 %collective-permute-start.1 = (s32[256]{0:T(256)}, s32[256]{0:T(256)S(1)}, u32[]{:S(2)}, u32[]{:S(2)}) collective-permute-start(s32[256]{0:T(256)} %bitcast.51), channel_id=1, source_target_pairs={{0,2},{2,4},{4,6},{6,8},{8,10},{10,12},{12,14},{14,16},{16,18},{18... | collective-permute-start | bytes 3080 | tf_op jit(solution)/shard_map/ppermute | solution.py:19
  11.7 6.1 %collective-permute-start = (s32[256]{0:T(256)}, s32[256]{0:T(256)S(1)}, u32[]{:S(2)}, u32[]{:S(2)}) collective-permute-start(s32[256]{0:T(256)} %bitcast.52), channel_id=1, source_target_pairs={{0,4},{2,6},{4,8},{6,10},{8,12},{10,14},{12,16},{14,18},{16,20},{1... | collective-permute-start | bytes 3080 | tf_op jit(solution)/shard_map/ppermute | solution.py:19
  96.6 1.5 copy-start.2
  96.6 1.5 copy-start.3
  98.0 8.3 %slice-start = ((f32[256,2048]{1,0:T(8,128)}), f32[256,1024]{1,0:T(8,128)S(1)}, s32[]{:S(2)}) async-start(f32[256,2048]{1,0:T(8,128)} %copy-done.2), calls=%async_computation.2 | async-start | bytes 2097152 | tf_op jit(solution)/shard_map/slice | solution.py:60
  100.7 6.9 %copy-start.4 = (f32[256,128]{1,0:T(8,128)S(1)}, f32[256,128]{1,0:T(8,128)}, u32[]{:S(2)}) copy-start(f32[256,128]{1,0:T(8,128)} %get-tuple-element.13) | copy-start | bytes 393220
  100.7 6.9 %copy-start.5 = (f32[256,128]{1,0:T(8,128)S(1)}, f32[256,128]{1,0:T(8,128)}, u32[]{:S(2)}) copy-start(f32[256,128]{1,0:T(8,128)} %get-tuple-element.14) | copy-start | bytes 393220
  100.7 13.2 %collective-permute-start.3 = (bf16[256,1024]{1,0:T(8,128)(2,1)}, bf16[256,1024]{1,0:T(8,128)(2,1)}, u32[]{:S(2)}, u32[]{:S(2)}) collective-permute-start(bf16[256,1024]{1,0:T(8,128)(2,1)} %pad_maximum_fusion), channel_id=1, source_target_pairs={{0,2},{2,4},{4,6},{6,8},{8,10},{10,12},{12,14},{14,16},{16,18},{18... | collective-permute-start | bytes 1572872 | tf_op jit(solution)/shard_map/ppermute | solution.py:19
  103.1 42.8 %collective-permute-start.2 = (bf16[256,1024]{1,0:T(8,128)(2,1)}, bf16[256,1024]{1,0:T(8,128)(2,1)}, u32[]{:S(2)}, u32[]{:S(2)}) collective-permute-start(bf16[256,1024]{1,0:T(8,128)(2,1)} %pad_maximum_fusion), channel_id=1, source_target_pairs={{0,4},{2,6},{4,8},{6,10},{8,12},{10,14},{12,16},{14,18},{16,20},{1... | collective-permute-start | bytes 1572872 | tf_op jit(solution)/shard_map/ppermute | solution.py:19
  148.5 2.5 %copy-start.6 = (bf16[256,2,2,128]{3,0,2,1:T(8,128)(2,1)S(1)}, bf16[256,2,2,128]{3,0,2,1:T(8,128)(2,1)}, u32[]{:S(2)}) copy-start(bf16[256,2,2,128]{3,0,2,1:T(8,128)(2,1)} %get-tuple-element.7) | copy-start | bytes 786436
  151.1 2.5 %copy-start.7 = (pred[256,768]{0,1:T(8,128)(4,1)S(1)}, pred[256,768]{0,1:T(8,128)(4,1)}, u32[]{:S(2)}) copy-start(pred[256,768]{0,1:T(8,128)(4,1)} %fusion.26) | copy-start | bytes 589828
  154.7 4.0 %copy-start.1 = (bf16[1,256,2304]{2,1,0:T(8,128)(2,1)S(1)}, bf16[1,256,2304]{2,1,0:T(8,128)(2,1)}, u32[]{:S(2)}) copy-start(bf16[1,256,2304]{2,1,0:T(8,128)(2,1)} %param.6) | copy-start | bytes 3538948
  154.7 4.0 %copy-start.8 = (f32[2304]{0:T(1024)S(1)}, f32[2304]{0:T(1024)}, u32[]{:S(2)}) copy-start(f32[2304]{0:T(1024)} %param.11) | copy-start | bytes 27652
Sparse Core Ops, SparseCore 0:
  9.6 81.6 all-gather.2
  93.6 58.4 all-gather.4
where the time goes:
time: 167 us
  waiting for transfers between devices  111 us (66%)
  between operations  13.7 us (8%)
  matrix products  12.8 us (8%)
  starting transfers between devices  12.5 us (7%)
  other arithmetic  10.6 us (6%)
  local copies, waits for them, and re-layouts  6.49 us (4%)
    all_gather x1, waiting for transfers between devices, per_device(): lax.all_gather(w_qkv, 'seq', axis=0, tiled=True)  72.1 us
    ppermute x4, waiting for transfers between devices, from_behind(): return lax.ppermute(block, axis, route)  37.4 us
    ppermute x4, starting transfers between devices, from_behind(): return lax.ppermute(block, axis, route)  12.5 us
    dot_general x1, matrix products, per_device(): jnp.dot(normed, lax.all_gather(w_qkv, 'seq', axis=0, tiled=True), preferr...  5.25 us
    dot_general x1, matrix products, per_device(): jnp.dot(attended, lax.all_gather(w_out, 'seq', axis=0, tiled=True), prefe...  3.96 us
  transfers between devices with their start and end apart: 6, of which 3 were waited for; matrix products, arithmetic and copies ran while one was open for 15% of the time, Pallas kernels for 0%

commit v1 on v0

--- a/solution.py
+++ b/solution.py
@@ -54,7 +54,11 @@
     widened = hidden_in[0].astype(jnp.float32)
     normed = rms_scale(widened, pre_gain).astype(jnp.bfloat16)
     projected = jnp.dot(
-        normed, lax.all_gather(w_qkv, "seq", axis=0, tiled=True), preferred_element_type=jnp.float32
+        normed,
+        jnp.concatenate(
+            lax.all_to_all(jnp.stack([w_qkv] * lax.axis_size("seq")), "seq", 0, 0), axis=0
+        ),
+        preferred_element_type=jnp.float32,
     )
     queries = rotary(
         projected[:, : Q_HEADS * HEAD].reshape(tok_rows, KV_HEADS, groups, HEAD), positions, 0

time: 167 us -> 308 us (1.84)
  waiting for transfers between devices: 111 us -> 242 us
  local copies, waits for them, and re-layouts: 6.49 us -> 12.4 us
  starting transfers between devices: 12.5 us -> 17.2 us
    ppermute x4, waiting for transfers between devices: 37.4 us -> 241 us  [from_behind(): return lax.ppermute(block, axis, route)]
    all_gather x1 -> x0, waiting for transfers between devices: 72.1 us -> none  [per_device(): lax.all_gather(w_qkv, 'seq', axis=0, tiled=True)]
    all_to_all x0 -> x1, starting transfers between devices: none -> 6.6 us  [per_device(): lax.all_to_all(jnp.stack([w_qkv] * lax.axis_size('seq')), 'seq', 0, 0)]
    another operation x0 -> x1, local copies, waits for them, and re-layouts: none -> 5.93 us  [per_device(): jnp.stack([w_qkv] * lax.axis_size('seq'))]
  transfers between devices with their start and end apart: 6 -> 6, of which waited for: 3 -> 4; matrix products, arithmetic and copies ran while one was open for 15% -> 8% of each run, Pallas kernels for 0% -> 0%
where the time goes in v1:
time: 308 us; the launch traced here: 307 us
  waiting for transfers between devices  242 us (79%)
  starting transfers between devices  17.2 us (6%)
  between operations  13.7 us (4%)
  matrix products  12.8 us (4%)
  local copies, waits for them, and re-layouts  12.4 us (4%)
  other arithmetic  9.3 us (3%)
    ppermute x4, waiting for transfers between devices, from_behind(): return lax.ppermute(block, axis, route)  241 us
    ppermute x4, starting transfers between devices, from_behind(): return lax.ppermute(block, axis, route)  10.6 us
    all_to_all x1, starting transfers between devices, per_device(): lax.all_to_all(jnp.stack([w_qkv] * lax.axis_size('seq')), 'seq', 0, 0)  6.6 us
  transfers between devices with their start and end apart: 6, of which 4 were waited for; matrix products, arithmetic and copies ran while one was open for 8% of the time, Pallas kernels for 0%

profile of v1, /device:TPU:17, one launch (start us, length us, event | category | flops | bytes accessed | tf_op | source)
XLA Modules:
  0.0 307.2 jit_solution(5206192615280531052)
XLA Ops:
  6.5 5.9 %stack.2 = bf16[16,144,2048]{2,1,0:T(8,128)(2,1)} broadcast(bf16[144,2048]{1,0:T(8,128)(2,1)} %param.9), dimensions={1,2} | broadcast | bytes 10027008 | tf_op jit(solution)/shard_map/stack | solution.py:59
  12.5 6.6 %all-to-all-start = ((bf16[16,144,2048]{2,1,0:T(8,128)(2,1)}), bf16[16,144,2048]{2,1,0:T(8,128)(2,1)}, u32[]{:S(2)}, u32[]{:S(2)}) async-start(bf16[16,144,2048]{2,1,0:T(8,128)(2,1)} %stack.2), calls=%async_computation | async-start | bytes 18874368 | tf_op jit(solution)/shard_map/all_to_all | solution.py:59
  19.8 3.4 %collective-permute-start.1 = (s32[256]{0:T(256)S(1)}, s32[256]{0:T(256)S(1)}, u32[]{:S(2)}, u32[]{:S(2)}) collective-permute-start(s32[256]{0:T(256)S(1)} %bitcast.59), channel_id=1, source_target_pairs={{0,2},{2,4},{4,6},{6,8},{8,10},{10,12},{12,14},{14,16},{16,18},{18... | collective-permute-start | bytes 3080 | tf_op jit(solution)/shard_map/ppermute | solution.py:19
  23.2 3.1 %collective-permute-start = (s32[256]{0:T(256)S(1)}, s32[256]{0:T(256)S(1)}, u32[]{:S(2)}, u32[]{:S(2)}) collective-permute-start(s32[256]{0:T(256)S(1)} %bitcast.60), channel_id=1, source_target_pairs={{0,4},{2,6},{4,8},{6,10},{8,12},{10,14},{12,16},{14,18},{16,20},{1... | collective-permute-start | bytes 3080 | tf_op jit(solution)/shard_map/ppermute | solution.py:19
  26.7 1.2 multiply_cosine_fusion
  27.9 31.1 %collective-permute-done.1 = s32[256]{0:T(256)S(1)} collective-permute-done((s32[256]{0:T(256)S(1)}, s32[256]{0:T(256)S(1)}, u32[]{:S(2)}, u32[]{:S(2)}) %collective-permute-start.1) | collective-permute-done | bytes 1056 | tf_op jit(solution)/shard_map/ppermute | solution.py:19
  59.1 192.9 %collective-permute-done = s32[256]{0:T(256)S(1)} collective-permute-done((s32[256]{0:T(256)S(1)}, s32[256]{0:T(256)S(1)}, u32[]{:S(2)}, u32[]{:S(2)}) %collective-permute-start) | collective-permute-done | bytes 1056 | tf_op jit(solution)/shard_map/ppermute | solution.py:19
  252.0 1.4 fusion.28
  253.4 5.2 %fusion.18 = f32[256,2048]{1,0:T(8,128)S(1)} fusion(bf16[2304,2048]{1,0:T(8,128)(2,1)} %bitcast.3, bf16[1,256,2304]{2,1,0:T(8,128)(2,1)S(1)} %copy-done, f32[2304]{0:T(1024)S(1)} %copy-done.10, f32[256]{0:T(256)S(1)} %add_rsqrt_fusion.1), kind=kOutput, calls=%fused_computation.20 | convolution fusion | flops 2418278400 | bytes 12724224 | tf_op jit(solution)/shard_map/dot_general | solution.py:56
  258.8 1.4 reshape.276
  260.2 1.4 subtract_convert_fusion.1
  262.8 2.0 collective-permute-start.3
  264.8 2.1 collective-permute-start.2
  266.9 0.9 reshape.278
  268.2 0.9 subtract_convert_fusion
  269.2 4.6 %collective-permute-done.3 = bf16[256,1024]{1,0:T(8,128)(2,1)} collective-permute-done((bf16[256,1024]{1,0:T(8,128)(2,1)}, bf16[256,1024]{1,0:T(8,128)(2,1)}, u32[]{:S(2)}, u32[]{:S(2)}) %collective-permute-start.3) | collective-permute-done | bytes 524320 | tf_op jit(solution)/shard_map/ppermute | solution.py:19
  273.8 12.3 %collective-permute-done.2 = bf16[256,1024]{1,0:T(8,128)(2,1)} collective-permute-done((bf16[256,1024]{1,0:T(8,128)(2,1)}, bf16[256,1024]{1,0:T(8,128)(2,1)}, u32[]{:S(2)}, u32[]{:S(2)}) %collective-permute-start.2) | collective-permute-done | bytes 524320 | tf_op jit(solution)/shard_map/ppermute | solution.py:19
  286.1 1.4 maximum_maximum_fusion
  287.5 1.2 reshape.277
  288.7 2.0 fusion.37
  291.2 2.4 fusion.6
  293.7 1.2 divide_convert_fusion
  294.9 4.0 %multiply_reduce_fusion = (f32[256]{0:T(256)S(1)}, f32[256,2304]{1,0:T(8,128)S(1)}) fusion(bf16[256,1024]{0,1:T(8,128)(2,1)S(1)} %bitcast.57, bf16[1024,2304]{1,0:T(8,128)(2,1)} %all-gather.2.cloned.1.call-done), kind=kOutput, calls=%fused_computation.9 | convolution fusion | flops 1209138944 | bytes 7603200 | tf_op jit(solution)/shard_map/dot_general | solution.py:96
  298.9 1.4 fusion.20
  (44 shorter events, 3.3 us)
Async XLA Ops:
  12.5 7.3 %copy-start.9 = (s32[1,256]{1,0:T(1,128)S(1)}, s32[1,256]{1,0:T(1,128)}, u32[]{:S(2)}) copy-start(s32[1,256]{1,0:T(1,128)} %param.7) | copy-start | bytes 3076
  12.5 13.9 %copy-start = (bf16[1,256,2304]{2,1,0:T(8,128)(2,1)S(1)}, bf16[1,256,2304]{2,1,0:T(8,128)(2,1)}, u32[]{:S(2)}) copy-start(bf16[1,256,2304]{2,1,0:T(8,128)(2,1)} %param.6) | copy-start | bytes 3538948
  12.5 240.9 %copy-start.10 = (f32[2304]{0:T(1024)S(1)}, f32[2304]{0:T(1024)}, u32[]{:S(2)}) copy-start(f32[2304]{0:T(1024)} %param.8) | copy-start | bytes 27652
  12.5 240.9 %all-to-all-start = ((bf16[16,144,2048]{2,1,0:T(8,128)(2,1)}), bf16[16,144,2048]{2,1,0:T(8,128)(2,1)}, u32[]{:S(2)}, u32[]{:S(2)}) async-start(bf16[16,144,2048]{2,1,0:T(8,128)(2,1)} %stack.2), calls=%async_computation | async-start | bytes 18874368 | tf_op jit(solution)/shard_map/all_to_all | solution.py:59
  19.1 275.8 %all-gather.2.cloned.1.call-start = ((), (), s32[]{:S(2)}) async-start(), calls=%async_computation.1 | async-start | bytes 5013504 | tf_op jit(solution)/shard_map/all_gather | solution.py:98
  19.8 39.3 %collective-permute-start.1 = (s32[256]{0:T(256)S(1)}, s32[256]{0:T(256)S(1)}, u32[]{:S(2)}, u32[]{:S(2)}) collective-permute-start(s32[256]{0:T(256)S(1)} %bitcast.59), channel_id=1, source_target_pairs={{0,2},{2,4},{4,6},{6,8},{8,10},{10,12},{12,14},{14,16},{16,18},{18... | collective-permute-start | bytes 3080 | tf_op jit(solution)/shard_map/ppermute | solution.py:19
  23.2 228.8 %collective-permute-start = (s32[256]{0:T(256)S(1)}, s32[256]{0:T(256)S(1)}, u32[]{:S(2)}, u32[]{:S(2)}) collective-permute-start(s32[256]{0:T(256)S(1)} %bitcast.60), channel_id=1, source_target_pairs={{0,4},{2,6},{4,8},{6,10},{8,12},{10,14},{12,16},{14,18},{16,20},{1... | collective-permute-start | bytes 3080 | tf_op jit(solution)/shard_map/ppermute | solution.py:19
  258.7 1.5 copy-start.2
  258.7 1.5 copy-start.3
  260.1 6.8 %slice-start = ((f32[256,2048]{1,0:T(8,128)}), f32[256,1024]{1,0:T(8,128)S(1)}, s32[]{:S(2)}) async-start(f32[256,2048]{1,0:T(8,128)} %copy-done.2), calls=%async_computation.2 | async-start | bytes 2097152 | tf_op jit(solution)/shard_map/slice | solution.py:64
  262.8 5.4 %copy-start.4 = (f32[256,128]{1,0:T(8,128)S(1)}, f32[256,128]{1,0:T(8,128)}, u32[]{:S(2)}) copy-start(f32[256,128]{1,0:T(8,128)} %get-tuple-element.13) | copy-start | bytes 393220
  262.8 5.5 %copy-start.5 = (f32[256,128]{1,0:T(8,128)S(1)}, f32[256,128]{1,0:T(8,128)}, u32[]{:S(2)}) copy-start(f32[256,128]{1,0:T(8,128)} %get-tuple-element.14) | copy-start | bytes 393220
  262.8 11.0 %collective-permute-start.3 = (bf16[256,1024]{1,0:T(8,128)(2,1)}, bf16[256,1024]{1,0:T(8,128)(2,1)}, u32[]{:S(2)}, u32[]{:S(2)}) collective-permute-start(bf16[256,1024]{1,0:T(8,128)(2,1)} %pad_maximum_fusion), channel_id=1, source_target_pairs={{0,2},{2,4},{4,6},{6,8},{8,10},{10,12},{12,14},{14,16},{16,18},{18... | collective-permute-start | bytes 1572872 | tf_op jit(solution)/shard_map/ppermute | solution.py:19
  264.8 21.3 %collective-permute-start.2 = (bf16[256,1024]{1,0:T(8,128)(2,1)}, bf16[256,1024]{1,0:T(8,128)(2,1)}, u32[]{:S(2)}, u32[]{:S(2)}) collective-permute-start(bf16[256,1024]{1,0:T(8,128)(2,1)} %pad_maximum_fusion), channel_id=1, source_target_pairs={{0,4},{2,6},{4,8},{6,10},{8,12},{10,14},{12,16},{14,18},{16,20},{1... | collective-permute-start | bytes 1572872 | tf_op jit(solution)/shard_map/ppermute | solution.py:19
  288.6 2.5 copy-start.6
  291.2 2.5 copy-start.7
  294.9 4.0 %copy-start.1 = (bf16[1,256,2304]{2,1,0:T(8,128)(2,1)S(1)}, bf16[1,256,2304]{2,1,0:T(8,128)(2,1)}, u32[]{:S(2)}) copy-start(bf16[1,256,2304]{2,1,0:T(8,128)(2,1)} %param.6) | copy-start | bytes 3538948
  294.9 4.0 %copy-start.8 = (f32[2304]{0:T(1024)S(1)}, f32[2304]{0:T(1024)}, u32[]{:S(2)}) copy-start(f32[2304]{0:T(1024)} %param.11) | copy-start | bytes 27652
Sparse Core Ops, SparseCore 0:
  22.2 164.0 all-gather.1
